TPU v7x, 128 devices: a whole 4x4x4 slice. The times are simulated.
128 devices in a mesh: narrow: 4 (over y), wide: 32 (over z, x, core).
Axes of the slice: x: 4, y: 4, z: 4, core: 2. Of those that a mesh axis runs over, the one named last changes fastest.
Arguments:
- level_set: float32 [1024, 256, 512], P('wide', 'narrow')
- velocity: bfloat16 [3, 1024, 256, 512], P(None, 'wide', 'narrow'), may hold values from -2 to 2
- box_owner: int32 [32, 4, 256, 1], P('wide', 'narrow'), may hold values from 0 to 31; in each aligned block of 256 rows (0 to 255, 256 to 511, ..., all dimensions but the last counted through in order) at most 20 rows name the same one
Outputs:
- surface: float32 [1024, 256, 512], P('wide', 'narrow')
- box_fractions: float32 [32, 4, 640, 512], P('wide', 'narrow')
Inputs may be any that keep to these rules, and one draw needn't show every extreme that they name: `box_owner`: the tiles of one device name one box owner at most 20 times.
All inputs are finite; a program needn't handle non-finite values.
Results may differ from a plain program's by a relative error of at most 0.0003.
Values sent between devices are 32-bit elements; how exact they have to be, the bound alone decides.
A program may use at most 192 MiB of HBM per device.

v0:
```python
import jax
import jax.numpy as jnp
from jax import lax
from jax.sharding import PartitionSpec as P

TILE = 16
SWEEPS = 3


WENO_EPS = 1e-06
PSEUDO_STEP = 0.3


def with_halo(shard, sides, width):
    edges = {}
    for axis, dim in sides:
        peers, length = (lax.axis_size(axis), shard.shape[dim])
        up = [(i, (i + 1) % peers) for i in range(peers)]
        last = lax.slice_in_dim(shard, length - width, length, axis=dim)
        first = lax.slice_in_dim(shard, 0, width, axis=dim)
        edges[dim] = (
            lax.ppermute(last, axis, up),
            lax.ppermute(first, axis, [(b, a) for a, b in up]),
        )
    done = []
    for _, dim in sides:
        low, high = edges[dim]
        around = [(width, width) if d in done else (0, 0) for d in range(shard.ndim)]
        shard = jnp.concatenate([jnp.pad(low, around), shard, jnp.pad(high, around)], axis=dim)
        done.append(dim)
    return shard


def extended(shard, sides, width):
    for axis, dim in sides:
        peers, length = (lax.axis_size(axis), shard.shape[dim])
        up = [(i, (i + 1) % peers) for i in range(peers)]
        down = [(j, i) for i, j in up]
        last = lax.slice_in_dim(shard, length - width, length, axis=dim)
        first = lax.slice_in_dim(shard, 0, width, axis=dim)
        before = lax.ppermute(last, axis, up)
        after = lax.ppermute(first, axis, down)
        shard = jnp.concatenate([before, shard, after], axis=dim)
    return shard


def weno_blend(parts):
    guesses = (
        parts[0] / 3.0 - 7.0 * parts[1] / 6.0 + 11.0 * parts[2] / 6.0,
        -parts[1] / 6.0 + 5.0 * parts[2] / 6.0 + parts[3] / 3.0,
        parts[2] / 3.0 + 5.0 * parts[3] / 6.0 - parts[4] / 6.0,
    )
    roughness = (
        13.0 / 12.0 * jnp.square(parts[0] - 2.0 * parts[1] + parts[2])
        + 0.25 * jnp.square(parts[0] - 4.0 * parts[1] + 3.0 * parts[2]),
        13.0 / 12.0 * jnp.square(parts[1] - 2.0 * parts[2] + parts[3])
        + 0.25 * jnp.square(parts[1] - parts[3]),
        13.0 / 12.0 * jnp.square(parts[2] - 2.0 * parts[3] + parts[4])
        + 0.25 * jnp.square(3.0 * parts[2] - 4.0 * parts[3] + parts[4]),
    )
    weights = [
        ideal_share / jnp.square(WENO_EPS + rough_part)
        for ideal_share, rough_part in zip((0.1, 0.6, 0.3), roughness)
    ]
    numerator = weights[0] * guesses[0] + weights[1] * guesses[1] + weights[2] * guesses[2]
    return numerator / (weights[0] + weights[1] + weights[2])


def weno_pair(padded, along):
    extent = padded.shape[along] - 6
    differences = jnp.diff(padded, axis=along)
    stencil = [
        lax.slice_in_dim(differences, offset, offset + extent, axis=along) for offset in range(6)
    ]
    from_below = weno_blend(stencil[0:5])
    from_above = weno_blend([stencil[5], stencil[4], stencil[3], stencil[2], stencil[1]])
    return (from_below, from_above)


def upwind(padded, along, speed):
    from_below, from_above = weno_pair(padded, along)
    return speed * jnp.where(speed > 0, from_below, from_above)


def advect_from(field, along_x, along_y, along_z, velocity):
    speeds = velocity.astype(jnp.float32)
    change = (
        upwind(along_x, 0, speeds[0])
        + upwind(along_y, 1, speeds[1])
        + upwind(along_z, 2, speeds[2])
    )
    return field - change


def godunov_sweep(rimmed, initial):
    center = rimmed[1:-1, 1:-1, :]
    column_pad = jnp.pad(center, ((0, 0), (0, 0), (1, 1)), mode="edge")
    smooth_sign = initial / jnp.sqrt(initial * initial + 1.0)
    outside = initial > 0

    def godunov(lower_side, upper_side):
        behind = center - lower_side
        forward = upper_side - center
        outer_term = jnp.maximum(
            jnp.square(jnp.maximum(behind, 0.0)), jnp.square(jnp.minimum(forward, 0.0))
        )
        inner_term = jnp.maximum(
            jnp.square(jnp.minimum(behind, 0.0)), jnp.square(jnp.maximum(forward, 0.0))
        )
        return jnp.where(outside, outer_term, inner_term)

    squared = godunov(rimmed[:-2, 1:-1, :], rimmed[2:, 1:-1, :])
    squared = squared + godunov(rimmed[1:-1, :-2, :], rimmed[1:-1, 2:, :])
    squared = squared + godunov(column_pad[:, :, :-2], column_pad[:, :, 2:])
    return center - PSEUDO_STEP * smooth_sign * (jnp.sqrt(squared) - 1.0)


def fraction(field):
    return 0.5 - 0.5 * field / jnp.sqrt(field * field + 1.0)


def to_tiles(one_block, edge):
    sizes_a, sizes_b, sizes_c = one_block.shape
    grouped = one_block.reshape(sizes_a // edge, edge, sizes_b // edge, edge, sizes_c // edge, edge)
    return grouped.transpose(0, 2, 4, 1, 3, 5).reshape(-1, edge**3)


def restrict(tiles, edge):
    leading = tiles.shape[:-1]
    half_edge = edge // 2
    depth = len(leading)
    grouped = tiles.reshape(leading + (half_edge, 2, half_edge, 2, half_edge, 2))
    return jnp.mean(grouped, axis=(depth + 1, depth + 3, depth + 5)).reshape(
        leading + (half_edge**3,)
    )


def pack_matrix(one_route, owners, capacity):
    owners_list = jnp.arange(owners, dtype=jnp.int32)
    matches = (one_route[:, None] == owners_list[None, :]).astype(jnp.int32)
    earlier = jnp.cumsum(matches, axis=0) - matches
    position = jnp.sum(earlier * matches, axis=1)
    target = one_route * capacity + position
    targets = jnp.arange(owners * capacity, dtype=jnp.int32)
    return (targets[:, None] == target[None, :]).astype(jnp.float32)


def on_device(level_set, velocity, box_owner):
    rimmed = with_halo(level_set, (("narrow", 1), ("wide", 0)), 3)
    along_x = rimmed[:, 3:-3, :]
    along_y = rimmed[3:-3, :, :]
    along_z = jnp.pad(level_set, ((0, 0), (0, 0), (3, 3)), mode="edge")
    moved = advect_from(level_set, along_x, along_y, along_z, velocity)
    wide_rim = extended(moved, (("narrow", 1), ("wide", 0)), SWEEPS)
    surface = wide_rim
    for sweep_index in range(SWEEPS):
        shrink = sweep_index + 1
        initial = wide_rim[
            shrink : wide_rim.shape[0] - shrink, shrink : wide_rim.shape[1] - shrink, :
        ]
        surface = godunov_sweep(surface, initial)
    liquid = fraction(surface)
    owners = lax.axis_size("wide")
    tile_count = box_owner.shape[2]
    capacity = max(2, 5 * tile_count // (2 * owners))
    matrix = pack_matrix(box_owner.reshape(-1), owners, capacity)
    coarse = restrict(to_tiles(liquid, TILE), TILE)
    outgoing = jnp.dot(
        matrix, coarse, precision=lax.Precision.HIGHEST, preferred_element_type=jnp.float32
    )
    outgoing = outgoing.reshape(owners, capacity, -1)
    box_slots = lax.all_to_all(outgoing, "wide", split_axis=0, concat_axis=0, tiled=True)
    return (surface, box_slots.reshape(1, 1, owners * capacity, -1))


def solution(mesh):
    return jax.shard_map(
        on_device,
        mesh=mesh,
        in_specs=(
            P("wide", "narrow", None),
            P(None, "wide", "narrow", None),
            P("wide", "narrow", None, None),
        ),
        out_specs=(P("wide", "narrow", None), P("wide", "narrow", None, None)),
        check_vma=False,
    )
```

profile of v0, /device:TPU:1, one launch (start us, length us, event | category | flops | bytes accessed | tf_op | source)
XLA Modules:
  0.0 263.4 jit_solution(11231233293891432093)
XLA Ops:
  0.6 2.0 fusion.17
  2.6 3.6 %collective-permute-start.2 = (f32[32,3,512]{2,1,0:T(4,128)}, f32[32,3,512]{2,1,0:T(4,128)S(1)}, u32[]{:S(2)}, u32[]{:S(2)}) collective-permute-start(f32[32,3,512]{2,1,0:T(4,128)} %get-tuple-element.17), channel_id=1, source_target_pairs={{32,0},{64,32},{96,64},{0,96},{33,1},{65,33},{97,65},{1,97},{34,2}... | collective-permute-start | bytes 589832 | tf_op jit(solution)/shard_map/ppermute | solution.py:23
  6.2 0.0 collective-permute-start.1
  6.2 2.1 fusion.16
  8.3 1.0 collective-permute-start.3
  9.2 1.1 collective-permute-start
  10.3 1.9 fusion.18
  12.2 0.4 copy.22
  12.6 0.4 copy.21
  13.0 0.3 reshape.74
  13.3 0.3 reshape.73
  13.7 0.0 slice-start.2
  13.7 4.0 %pad_maximum_fusion.3 = f32[32,64,518]{2,1,0:T(8,128)S(1)} fusion(f32[32,64,3]{2,1,0:T(8,128)S(1)} %reshape.74, f32[32,64,512]{2,1,0:T(8,128)} %param.3, f32[32,64,3]{2,1,0:T(8,128)S(1)} %reshape.73), kind=kLoop, calls=%fused_computation.16 | loop fusion | flops 2121728 | bytes 8486912 | tf_op jit(solution)/shard_map/jit(_pad)/concatenate | solution.py:152
  17.7 0.0 copy-start.1
  17.7 0.0 slice-start.3
  17.7 3.7 %slice_subtract_fusion.4 = f32[32,64,517]{2,1,0:T(8,128)} fusion(f32[32,64,518]{2,1,0:T(8,128)S(1)} %pad_maximum_fusion.3), kind=kLoop, calls=%fused_computation.15 | loop fusion | flops 1058816 | bytes 12705792 | tf_op jit(solution)/shard_map/jit(diff)/sub | solution.py:71
  21.4 0.0 copy-done.1
  21.5 0.0 slice-done.2
  21.5 0.0 slice-done.3
  21.5 6.4 %convert_element_type.14 = f32[3,32,64,512]{3,2,1,0:T(8,128)} convert(bf16[3,32,64,512]{3,2,1,0:T(8,128)(2,1)S(1)} %bitcast.46) | non-fusion elementwise | flops 3145728 | bytes 18874368 | tf_op jit(solution)/shard_map/convert_element_type | solution.py:86
  27.9 0.6 reduce-window.6
  28.5 0.2 slice_reduce_fusion
  28.7 0.0 collective-permute-done.2
  28.7 0.0 collective-permute-done.1
  28.7 2.9 %pad_maximum_fusion.6 = f32[32,70,512]{2,1,0:T(8,128)S(1)} fusion(f32[32,3,512]{2,1,0:T(4,128)S(1)} %collective-permute-done.2, f32[32,64,512]{2,1,0:T(8,128)} %param.3, f32[32,3,512]{2,1,0:T(4,128)S(1)} %collective-permute-done.1), kind=kLoop, calls=%fused_computation.28 | loop fusion | flops 2293760 | bytes 9175040 | tf_op jit(solution)/shard_map/concatenate | solution.py:29
  31.6 0.0 copy-start
  31.6 0.7 slice_subtract_fusion.10
  32.4 0.0 collective-permute-done.3
  32.4 0.0 collective-permute-done
  32.4 1.4 copy-done
  33.8 2.2 select_maximum_fusion
  36.0 0.0 slice-start.1
  36.0 1.0 slice_subtract_fusion.9
  37.0 0.3 slice-done.1
  37.3 58.8 %add_subtract_fusion = f32[32,64,512]{2,1,0:T(8,128)S(1)} fusion(f32[32,64,512]{2,1,0:T(8,128)S(1)} %copy-done, f32[32,64,517]{2,1,0:T(8,128)S(1)} %bitcast.43, f32[32,69,512]{2,1,0:T(8,128)S(1)} %slice_subtract_fusion.10, f32[37,64,512]{2,1,0:T(8,128)S(1)} %slice_subtract_fusion.9, f32[3,32,64,512]{3,2,1,0:T(8,128)} %convert_element_type.14), kind=kLoop, calls=%fused_computation.42 | loop fusion | flops 402653184 | bytes 96468992 | tf_op jit(solution)/shard_map/sub | solution.py:92
  96.1 0.1 fusion.15
  96.2 3.2 %collective-permute-start.5 = (f32[32,3,512]{2,1,0:T(4,128)S(1)}, f32[32,3,512]{2,1,0:T(4,128)S(1)}, u32[]{:S(2)}, u32[]{:S(2)}) collective-permute-start(f32[32,3,512]{2,1,0:T(4,128)S(1)} %get-tuple-element.13), channel_id=1, source_target_pairs={{32,0},{64,32},{96,64},{0,96},{33,1},{65,33},{97,65},{1,97},{34,2}... | collective-permute-start | bytes 589832 | tf_op jit(solution)/shard_map/ppermute | solution.py:42
  99.4 0.0 collective-permute-start.4
  99.4 0.1 fusion.10
  99.5 3.2 %collective-permute-done.5 = f32[32,3,512]{2,1,0:T(4,128)S(1)} collective-permute-done((f32[32,3,512]{2,1,0:T(4,128)S(1)}, f32[32,3,512]{2,1,0:T(4,128)S(1)}, u32[]{:S(2)}, u32[]{:S(2)}) %collective-permute-start.5) | collective-permute-done | bytes 196640 | tf_op jit(solution)/shard_map/ppermute | solution.py:42
  102.7 3.1 %collective-permute-done.4 = f32[32,3,512]{2,1,0:T(4,128)S(1)} collective-permute-done((f32[32,3,512]{2,1,0:T(4,128)S(1)}, f32[32,3,512]{2,1,0:T(4,128)S(1)}, u32[]{:S(2)}, u32[]{:S(2)}) %collective-permute-start.4) | collective-permute-done | bytes 196640 | tf_op jit(solution)/shard_map/ppermute | solution.py:41
  105.9 0.1 pad_maximum_fusion.11
  106.0 5.5 %collective-permute-start.7 = (f32[3,70,512]{2,1,0:T(8,128)S(1)}, f32[3,70,512]{2,1,0:T(8,128)S(1)}, u32[]{:S(2)}, u32[]{:S(2)}) collective-permute-start(f32[3,70,512]{2,1,0:T(8,128)S(1)} %get-tuple-element.11), channel_id=1, source_target_pairs={{1,0},{2,1},{3,2},{4,3},{5,4},{6,5},{7,6},{8,7},{9,8},{10,9},{11,1... | collective-permute-start | bytes 1290248 | tf_op jit(solution)/shard_map/ppermute | solution.py:42
  111.5 0.0 collective-permute-start.6
  111.5 0.2 broadcast_compare_fusion
  111.7 5.0 %collective-permute-done.7 = f32[3,70,512]{2,1,0:T(8,128)S(1)} collective-permute-done((f32[3,70,512]{2,1,0:T(8,128)S(1)}, f32[3,70,512]{2,1,0:T(8,128)S(1)}, u32[]{:S(2)}, u32[]{:S(2)}) %collective-permute-start.7) | collective-permute-done | bytes 430112 | tf_op jit(solution)/shard_map/ppermute | solution.py:42
  116.7 0.1 collective-permute-done.6
  116.8 0.9 pad_maximum_fusion
  117.6 0.8 slice.333
  118.4 0.5 fusion.12
  118.9 12.3 %multiply_subtract_fusion = f32[36,68,512]{2,1,0:T(8,128)S(1)} fusion(f32[36,68,512]{2,1,0:T(8,128)S(1)} %slice.333, f32[36,68,1]{2,1,0:T(8,128)S(1)} %get-tuple-element.5, f32[36,68,1]{2,1,0:T(8,128)S(1)} %get-tuple-element.4, f32[38,70,512]{2,1,0:T(8,128)S(1)} %pad_maximum_fusion), kind=kLoop, calls=%fused_computation.13 | loop fusion | flops 63922176 | bytes 30100608 | tf_op jit(solution)/shard_map/sub | solution.py:115
  131.3 0.7 slice.340
  132.0 0.5 fusion.13
  132.5 12.3 %multiply_subtract_fusion.1 = f32[34,66,512]{2,1,0:T(8,128)S(1)} fusion(f32[34,66,512]{2,1,0:T(8,128)S(1)} %slice.340, f32[34,66,1]{2,1,0:T(8,128)S(1)} %get-tuple-element.7, f32[34,66,1]{2,1,0:T(8,128)S(1)} %get-tuple-element.6, f32[36,68,512]{2,1,0:T(8,128)S(1)} %multiply_subtract_fusion, f32[38,70,512]{2,1,0:T(8,128)S(1)} %pad_maximum_fusion), kind=kLoop, calls=%fused_computation.25 | loop fusion | flops 58595328 | bytes 32187936 | tf_op jit(solution)/shard_map/sub | solution.py:115
  144.8 0.8 slice.348
  145.5 0.4 fusion.14
  146.0 11.7 %multiply_subtract_fusion.2 = (f32[32,64,512]{2,1,0:T(8,128)}, f32[32,64,512]{2,1,0:T(8,128)}) fusion(f32[32,64,512]{2,1,0:T(8,128)S(1)} %slice.348, f32[32,64,1]{2,1,0:T(8,128)S(1)} %get-tuple-element.9, f32[32,64,1]{2,1,0:T(8,128)S(1)} %get-tuple-element.8, f32[34,66,512]{2,1,0:T(8,128)S(1)} %multiply_subtract_fusion.1, f32[32,64,512]{2,1,0:T(8,128)S(1)} %add_subtract_fusion), kind=kLoop, calls=%fused_computation.40 | loop fusion | flops 58720256 | bytes 33570816 | tf_op jit(solution)/shard_map/sub | solution.py:119
  157.7 19.8 %reshape.77 = f32[2,16,4,16,32,16]{5,4,3,2,1,0:T(8,128)} reshape(f32[32,64,512]{2,1,0:T(8,128)} %get-tuple-element.2) | data formatting | bytes 8388608 | tf_op jit(solution)/shard_map/reshape | solution.py:124
  177.5 27.6 %copy.14 = f32[2,4,32,16,16,16]{2,1,0,5,4,3:T(4,128)} copy(f32[2,4,32,16,16,16]{5,2,4,1,3,0:T(8,128)} %bitcast.44) | data formatting | bytes 8388608 | tf_op jit(solution)/shard_map/transpose | solution.py:125
  205.2 16.0 %reshape_reshape.3 = f32[256,8,2,8,2,8,2]{0,6,5,4,3,2,1:T(2,128)} reshape(f32[2,4,32,16,16,16]{2,1,0,5,4,3:T(4,128)} %copy.14) | data formatting | bytes 8388608 | tf_op jit(solution)/shard_map/reshape;reshape | solution.py:132
  221.2 4.9 %reduce_sum.19 = f32[256,8,8,8]{0,3,2,1:T(8,128)S(1)} reduce(f32[256,8,2,8,2,8,2]{0,6,5,4,3,2,1:T(2,128)} %reshape_reshape.3, f32[]{:T(128)} %constant.96.clone.1), dimensions={2,4,6}, to_apply=%region_3.4 | reduce | flops 917504 | bytes 4718596 | tf_op jit(solution)/shard_map/reduce_sum | solution.py:133
  226.2 0.9 fusion.6
  227.1 35.1 %all_to_all.5 = f32[32,20,512]{2,1,0:T(8,128)S(1)} all-to-all(f32[32,20,512]{2,1,0:T(8,128)S(1)} %fusion.6), channel_id=1, replica_groups=mesh['narrow'=4,'wide'=32] {'wide'}, dimensions={0} | all-to-all | bytes 2621440 | tf_op jit(solution)/shard_map/all_to_all | solution.py:172
  262.2 1.2 reshape.78
  (13 shorter events, 0.1 us)
Async XLA Ops:
  2.6 26.1 %collective-permute-start.2 = (f32[32,3,512]{2,1,0:T(4,128)}, f32[32,3,512]{2,1,0:T(4,128)S(1)}, u32[]{:S(2)}, u32[]{:S(2)}) collective-permute-start(f32[32,3,512]{2,1,0:T(4,128)} %get-tuple-element.17), channel_id=1, source_target_pairs={{32,0},{64,32},{96,64},{0,96},{33,1},{65,33},{97,65},{1,97},{34,2}... | collective-permute-start | bytes 589832 | tf_op jit(solution)/shard_map/ppermute | solution.py:23
  6.2 22.5 %collective-permute-start.1 = (f32[32,3,512]{2,1,0:T(4,128)S(1)}, f32[32,3,512]{2,1,0:T(4,128)S(1)}, u32[]{:S(2)}, u32[]{:S(2)}) collective-permute-start(f32[32,3,512]{2,1,0:T(4,128)S(1)} %get-tuple-element.16), channel_id=1, source_target_pairs={{0,32},{32,64},{64,96},{96,0},{1,33},{33,65},{65,97},{97,1},{2,34}... | collective-permute-start | bytes 589832 | tf_op jit(solution)/shard_map/ppermute | solution.py:22
  8.3 24.1 %collective-permute-start.3 = (f32[3,64,512]{2,1,0:T(8,128)}, f32[3,64,512]{2,1,0:T(8,128)S(1)}, u32[]{:S(2)}, u32[]{:S(2)}) collective-permute-start(f32[3,64,512]{2,1,0:T(8,128)} %get-tuple-element.15), channel_id=1, source_target_pairs={{1,0},{2,1},{3,2},{4,3},{5,4},{6,5},{7,6},{8,7},{9,8},{10,9},{11,1... | collective-permute-start | bytes 1179656 | tf_op jit(solution)/shard_map/ppermute | solution.py:23
  9.2 23.2 %collective-permute-start = (f32[3,64,512]{2,1,0:T(8,128)}, f32[3,64,512]{2,1,0:T(8,128)}, u32[]{:S(2)}, u32[]{:S(2)}) collective-permute-start(f32[3,64,512]{2,1,0:T(8,128)} %get-tuple-element.14), channel_id=1, source_target_pairs={{0,1},{1,2},{2,3},{3,4},{4,5},{5,6},{6,7},{7,8},{8,9},{9,10},{10,1... | collective-permute-start | bytes 1179656 | tf_op jit(solution)/shard_map/ppermute | solution.py:22
  13.7 7.8 %slice-start.2 = ((s8[6291456]{0:T(1024)(128)(4,1)}), s8[4194304]{0:T(1024)(128)(4,1)S(1)}, s32[]{:S(2)}) async-start(s8[6291456]{0:T(1024)(128)(4,1)} %bitcast.45), calls=%async_computation.3 | async-start | bytes 8388608
  17.7 3.7 %copy-start.1 = (s32[1,1,256,1]{2,3,1,0:T(1,128)S(1)}, s32[1,1,256,1]{2,3,1,0:T(1,128)}, u32[]{:S(2)}) copy-start(s32[1,1,256,1]{2,3,1,0:T(1,128)} %param.5) | copy-start | bytes 3076
  17.7 3.7 %slice-start.3 = ((s8[6291456]{0:T(1024)(128)(4,1)}), s8[2097152]{0:T(1024)(128)(4,1)S(1)}, s32[]{:S(2)}) async-start(s8[6291456]{0:T(1024)(128)(4,1)} %bitcast.45), calls=%async_computation.4 | async-start | bytes 4194304
  28.7 2.9 %copy-start.2 = (s32[32,3]{0,1:T(4,128)}, s32[32,3]{0,1:T(4,128)S(1)}, u32[]{:S(2)}) copy-start(s32[32,3]{0,1:T(4,128)S(1)} %reduce-window.9) | copy-start | bytes 1156
  31.6 2.2 copy-start
  33.8 3.2 %slice-start = ((s8[5242880]{0:T(1024)(128)(4,1)}), s8[4194304]{0:T(1024)(128)(4,1)S(1)}, s32[]{:S(2)}) async-start(s8[5242880]{0:T(1024)(128)(4,1)} %bitcast.42), calls=%async_computation.1 | async-start | bytes 8388608
  36.0 1.3 slice-start.1
  37.3 62.1 %slice-start.4 = ((s32[32,3]{0,1:T(4,128)}), s32[32,2]{0,1:T(2,128)S(1)}, s32[]{:S(2)}) async-start(s32[32,3]{0,1:T(4,128)} %copy-done.2), calls=%async_computation.5 | async-start | bytes 2048 | tf_op jit(solution)/shard_map/slice.19
  96.2 6.5 %collective-permute-start.5 = (f32[32,3,512]{2,1,0:T(4,128)S(1)}, f32[32,3,512]{2,1,0:T(4,128)S(1)}, u32[]{:S(2)}, u32[]{:S(2)}) collective-permute-start(f32[32,3,512]{2,1,0:T(4,128)S(1)} %get-tuple-element.13), channel_id=1, source_target_pairs={{32,0},{64,32},{96,64},{0,96},{33,1},{65,33},{97,65},{1,97},{34,2}... | collective-permute-start | bytes 589832 | tf_op jit(solution)/shard_map/ppermute | solution.py:42
  99.4 6.4 %collective-permute-start.4 = (f32[32,3,512]{2,1,0:T(4,128)S(1)}, f32[32,3,512]{2,1,0:T(4,128)S(1)}, u32[]{:S(2)}, u32[]{:S(2)}) collective-permute-start(f32[32,3,512]{2,1,0:T(4,128)S(1)} %get-tuple-element.12), channel_id=1, source_target_pairs={{0,32},{32,64},{64,96},{96,0},{1,33},{33,65},{65,97},{97,1},{2,34}... | collective-permute-start | bytes 589832 | tf_op jit(solution)/shard_map/ppermute | solution.py:41
  106.0 10.7 %collective-permute-start.7 = (f32[3,70,512]{2,1,0:T(8,128)S(1)}, f32[3,70,512]{2,1,0:T(8,128)S(1)}, u32[]{:S(2)}, u32[]{:S(2)}) collective-permute-start(f32[3,70,512]{2,1,0:T(8,128)S(1)} %get-tuple-element.11), channel_id=1, source_target_pairs={{1,0},{2,1},{3,2},{4,3},{5,4},{6,5},{7,6},{8,7},{9,8},{10,9},{11,1... | collective-permute-start | bytes 1290248 | tf_op jit(solution)/shard_map/ppermute | solution.py:42
  111.5 5.3 %collective-permute-start.6 = (f32[3,70,512]{2,1,0:T(8,128)S(1)}, f32[3,70,512]{2,1,0:T(8,128)S(1)}, u32[]{:S(2)}, u32[]{:S(2)}) collective-permute-start(f32[3,70,512]{2,1,0:T(8,128)S(1)} %get-tuple-element.10), channel_id=1, source_target_pairs={{0,1},{1,2},{2,3},{3,4},{4,5},{5,6},{6,7},{7,8},{8,9},{9,10},{10,1... | collective-permute-start | bytes 1290248 | tf_op jit(solution)/shard_map/ppermute | solution.py:41
where the time goes:
time: 265 us; the launch traced here: 263 us
  other arithmetic  123 us (46%)
  local copies, waits for them, and re-layouts  77.9 us (29%)
  blocking collectives  35.1 us (13%)
  starting transfers between devices  14.3 us (5%)
  waiting for transfers between devices  11.4 us (4%)
    sub x1, other arithmetic, advect_from(): return field - change  58.8 us
    all_to_all x1, blocking collectives, on_device(): lax.all_to_all(outgoing, 'wide', split_axis=0, concat_axis=0, tiled=True)  35.1 us
    transpose x1, local copies, waits for them, and re-layouts, to_tiles(): return grouped.transpose(0, 2, 4, 1, 3, 5).reshape(-1, edge ** 3)  27.6 us
    sub x2, other arithmetic, godunov_sweep(): return center - PSEUDO_STEP * smooth_sign * (jnp.sqrt(squared) - 1.0)  24.6 us
    reshape x1, local copies, waits for them, and re-layouts, to_tiles(): one_block.reshape(sizes_a // edge, edge, sizes_b // edge, edge, sizes_c /...  19.8 us
    another operation x1, local copies, waits for them, and re-layouts, restrict(): tiles.reshape(leading + (half_edge, 2, half_edge, 2, half_edge, 2))  16 us
    sub x1, other arithmetic, fraction(): return 0.5 - 0.5 * field / jnp.sqrt(field * field + 1.0)  11.7 us
    ppermute x2, starting transfers between devices, extended(): after = lax.ppermute(first, axis, down)  8.72 us
  transfers between devices with their start and end apart: 8, of which 4 were waited for; matrix products, arithmetic and copies ran while one was open for 9% of the time, Pallas kernels for 0%

commit v1 on v0

v1 whole, which is shorter than its diff:
```python
import functools

import jax
import jax.numpy as jnp
from jax import lax
from jax.experimental import pallas as pl
from jax.experimental.pallas import tpu as pltpu
from jax.sharding import PartitionSpec as P

f32 = jnp.float32
EPS = 0.75e-6
CX, CY, CZ = 32, 64, 512
CAP = 20
FIELD = (38, 4, 80, 128)
HIGH = lax.Precision.HIGHEST


def lanes_iota():
    return lax.broadcasted_iota(jnp.int32, (8, 128), 1)


def lane_from(prev, cur, k, lane):
    return pltpu.roll(jnp.where(lane >= 128 - k, prev, cur), k, 1)


def lane_to(cur, nxt, k, lane):
    return pltpu.roll(jnp.where(lane < k, nxt, cur), 128 - k, 1)


def corr(E1, E2, E3, E4):
    E2s = 0.75 * E2
    E3s = 0.75 * E3
    t1 = E2 - E1
    S1 = t1 * t1 + (E2s * (t1 + E2) + EPS)
    t2 = E3 - E2
    S2 = t2 * t2 + (E2s * E3 + EPS)
    t3 = E3 - E4
    S3 = t3 * t3 + (E3s * (t3 + E3) + EPS)
    r1 = 1.0 / S1
    r2 = 1.0 / S2
    r3 = 1.0 / S3
    w1 = r1 * r1
    w2 = (6.0 * r2) * r2
    w3 = (3.0 * r3) * r3
    return (E2 + (E3 + E3)) - ((w1 + w1) * (t2 - t1) - w3 * (t2 + t3)) / (w1 + w2 + w3)


def upwind(u, dm, dp, qm2, qm1, q0, qp1, qp2):
    p = u > 0
    V3 = jnp.where(p, dm, dp)
    E1 = jnp.where(p, qm2, qp2)
    E2 = jnp.where(p, qm1, qp1)
    E4 = jnp.where(p, qp1, qm1)
    return u * V3 + (jnp.abs(u) * (1.0 / 6.0)) * corr(E1, E2, q0, E4)


def differences(fs):
    d = [fs[i + 1] - fs[i] for i in range(6)]
    q = [d[i + 1] - d[i] for i in range(5)]
    return (d[2], d[3], *q)


def advect_group(x, row, F, V, M):
    lane = lanes_iota()
    zero = jnp.zeros((8, 128), f32)
    for h in range(2):
        r = row + 8 * h + 8
        fc = [F[x + 3, c, pl.ds(r, 8), :] for c in range(4)]
        dm, dp, q = [], [], []
        for c in range(4):
            if c > 0:
                fm = lane_from(fc[c - 1], fc[c], 1, lane)
            else:
                fm = jnp.where(lane == 0, fc[0], pltpu.roll(fc[0], 1, 1))
            if c < 3:
                fp = lane_to(fc[c], fc[c + 1], 1, lane)
            else:
                fp = jnp.where(lane == 127, fc[3], pltpu.roll(fc[3], 127, 1))
            dm.append(fc[c] - fm)
            dp.append(fp - fc[c])
            q.append(dp[c] - dm[c])
        for c in range(4):
            u = V[:, x, pl.ds(row, 16), c * 128 : c * 128 + 128][:, 8 * h : 8 * h + 8].astype(f32)
            fx = [fc[c] if k == 3 else F[x + k, c, pl.ds(r, 8), :] for k in range(7)]
            acc = upwind(u[0], *differences(fx))
            fy = [fc[c] if k == 3 else F[x + 3, c, pl.ds(r + k - 3, 8), :] for k in range(7)]
            acc = acc + upwind(u[1], *differences(fy))
            qp = q[c - 1] if c > 0 else zero
            qn = q[c + 1] if c < 3 else zero
            acc = acc + upwind(
                u[2],
                dm[c],
                dp[c],
                lane_from(qp, q[c], 2, lane),
                lane_from(qp, q[c], 1, lane),
                q[c],
                lane_to(q[c], qn, 1, lane),
                lane_to(q[c], qn, 2, lane),
            )
            M[x + 3, c, pl.ds(r, 8), :] = fc[c] - acc


def pack_rows(field, buf):
    def body(k, _):
        for j in range(8):
            for c in range(4):
                for s, row in ((0, 8), (1, 69)):
                    buf[s, c, pl.ds(k * 24 + 3 * j, 3), :] = field[k * 8 + j + 3, c, row : row + 3, :]
        return 0

    lax.fori_loop(0, 4, body, 0)


def unpack_rows(field, buf):
    def body(k, _):
        for j in range(8):
            for c in range(4):
                for s, row in ((0, 5), (1, 72)):
                    field[k * 8 + j + 3, c, row : row + 3, :] = buf[s, c, pl.ds(k * 24 + 3 * j, 3), :]
        return 0

    lax.fori_loop(0, 4, body, 0)


def advect_kernel(
    nw, nn, l_ref, v_ref, m_ref, F, M, V, ys, yr, ys2, yr2, cr, lsem, vsem, osem, ssem, rsem
):
    w, n = lax.axis_index("wide"), lax.axis_index("narrow")
    left, right = lax.rem(w + nw - 1, nw), lax.rem(w + 1, nw)
    down, up = lax.rem(n + nn - 1, nn), lax.rem(n + 1, nn)

    loads = [
        pltpu.make_async_copy(
            l_ref.at[:, :, c * 128 : c * 128 + 128], F.at[3:35, c, 8:72, :], lsem.at[c]
        )
        for c in range(4)
    ]
    speeds = [
        pltpu.make_async_copy(v_ref.at[:, a:b], V.at[:, a:b], vsem.at[i])
        for i, (a, b) in enumerate(((3, 16), (0, 3), (16, 32)))
    ]
    for copy in loads + speeds:
        copy.start()

    barrier = pltpu.get_barrier_semaphore()
    around = [(a, b) for a in (left, w, right) for b in (down, n, up)]
    del around[4]
    for a, b in around:
        pl.semaphore_signal(
            barrier, inc=1, device_id={"wide": a, "narrow": b}, device_id_type=pl.DeviceIdType.MESH
        )
    pl.semaphore_wait(barrier, 8)

    def send(src, dst, k, a, b):
        return pltpu.make_async_remote_copy(
            src_ref=src,
            dst_ref=dst,
            send_sem=ssem.at[k],
            recv_sem=rsem.at[k],
            device_id={"wide": a, "narrow": b},
            device_id_type=pl.DeviceIdType.MESH,
        )

    def sides(field, sent, got, k):
        return (
            [
                send(field.at[3:6, :, 8:72, :], field.at[35:38, :, 8:72, :], k, left, n),
                send(field.at[32:35, :, 8:72, :], field.at[0:3, :, 8:72, :], k + 1, right, n),
            ],
            [
                send(sent.at[0], got.at[1], k + 2, w, down),
                send(sent.at[1], got.at[0], k + 3, w, up),
            ],
        )

    first_x, first_y = sides(F, ys, yr, 0)
    second_x, second_y = sides(M, ys2, yr2, 4)
    corners = [
        send(ys2.at[0, :, 0:16, :], cr.at[1, 1], 8, left, down),
        send(ys2.at[1, :, 0:16, :], cr.at[1, 0], 9, left, up),
        send(ys2.at[0, :, 80:96, :], cr.at[0, 1], 10, right, down),
        send(ys2.at[1, :, 80:96, :], cr.at[0, 0], 11, right, up),
    ]

    for copy in loads:
        copy.wait()
    for copy in first_x:
        copy.start()
    pack_rows(F, ys)
    for copy in first_y:
        copy.start()

    def inner(i, _):
        advect_group(3 + i // 2, pl.multiple_of(16 + 16 * (i % 2), 16), F, V, M)
        return 0

    def rims(i, _):
        advect_group(i // 2, pl.multiple_of(48 * (i % 2), 16), F, V, M)
        return 0

    def ends(i, _):
        k = i // 2
        advect_group(k + 26 * (k // 3), pl.multiple_of(16 + 16 * (i % 2), 16), F, V, M)
        return 0

    speeds[0].wait()
    lax.fori_loop(0, 26, inner, 0)
    speeds[1].wait()
    speeds[2].wait()
    for copy in first_x + first_y:
        copy.wait()
    unpack_rows(F, yr)
    lax.fori_loop(0, 64, rims, 0)
    pack_rows(M, ys2)
    for copy in second_y + corners:
        copy.start()
    lax.fori_loop(0, 12, ends, 0)
    for copy in second_x:
        copy.start()
    outs = []

    def put(k, a, b, rows):
        rows = slice(*rows)
        copy = pltpu.make_async_copy(M.at[a:b, :, rows, :], m_ref.at[a:b, :, rows, :], osem.at[k])
        copy.start()
        outs.append(copy)

    put(0, 3, 19, (8, 72))
    lax.fori_loop(26, 52, inner, 0)
    put(1, 19, 35, (8, 72))
    for copy in second_x + second_y + corners:
        copy.wait()
    unpack_rows(M, yr2)
    for xs in range(2):
        for ysd in range(2):
            for j in range(3):
                row = (5, 72)[ysd]
                at = (7, 0)[xs] + 3 * j
                for c in range(4):
                    M[35 * xs + j, c, row : row + 3, :] = cr[xs, ysd, c, at : at + 3, :]
    put(2, 0, 3, (8, 72))
    put(3, 35, 38, (8, 72))
    put(4, 0, 38, (0, 8))
    put(5, 0, 38, (72, 80))
    for copy in outs:
        copy.wait()


def advect(level_set, velocity, nw, nn):
    return pl.pallas_call(
        functools.partial(advect_kernel, nw, nn),
        out_shape=jax.ShapeDtypeStruct(FIELD, f32),
        in_specs=[pl.BlockSpec(memory_space=pl.ANY)] * 2,
        out_specs=pl.BlockSpec(memory_space=pl.ANY),
        scratch_shapes=[
            pltpu.VMEM(FIELD, f32),
            pltpu.VMEM(FIELD, f32),
            pltpu.VMEM((3, CX, CY, CZ), jnp.bfloat16),
            pltpu.VMEM((2, 4, 96, 128), f32),
            pltpu.VMEM((2, 4, 96, 128), f32),
            pltpu.VMEM((2, 4, 96, 128), f32),
            pltpu.VMEM((2, 4, 96, 128), f32),
            pltpu.VMEM((2, 2, 4, 16, 128), f32),
            pltpu.SemaphoreType.DMA((4,)),
            pltpu.SemaphoreType.DMA((3,)),
            pltpu.SemaphoreType.DMA((6,)),
            pltpu.SemaphoreType.DMA((12,)),
            pltpu.SemaphoreType.DMA((12,)),
        ],
        compiler_params=pltpu.CompilerParams(
            collective_id=0, has_side_effects=True, vmem_limit_bytes=48 << 20
        ),
        name="advect",
    )(level_set, velocity)


def sweep_block(x, r, src, dst, S, lane, moved=None):
    fc = [src[x, c, pl.ds(r, 8), :] for c in range(4)]
    new = []
    for c in range(4):
        cur = fc[c]
        if moved is None:
            s = S[x, c, pl.ds(r, 8), :]
        else:
            s = (0.3 * cur) * lax.rsqrt(cur * cur + 1.0)
            S[x, c, pl.ds(r, 8), :] = s
        sg = jnp.where(s > 0, 1.0, -1.0)
        sc = sg * cur

        def term(lo, hi):
            e = sc - jnp.minimum(jnp.minimum(sg * lo, sg * hi), sc)
            return e * e

        G = term(src[x - 1, c, pl.ds(r, 8), :], src[x + 1, c, pl.ds(r, 8), :])
        G = G + term(src[x, c, pl.ds(r - 1, 8), :], src[x, c, pl.ds(r + 1, 8), :])
        if c > 0:
            lo = lane_from(fc[c - 1], cur, 1, lane)
        else:
            lo = jnp.where(lane == 0, cur, pltpu.roll(cur, 1, 1))
        if c < 3:
            hi = lane_to(cur, fc[c + 1], 1, lane)
        else:
            hi = jnp.where(lane == 127, cur, pltpu.roll(cur, 127, 1))
        G = G + term(lo, hi)
        root = G * lax.rsqrt(jnp.maximum(G, 1e-37))
        new.append(cur - s * (root - 1.0))
    return new


def sweep_kernel(nw, m_ref, route_ref, surf_ref, out_ref, M, A, B, S, O, H, Q, C, msem, osem):
    loads = [
        pltpu.make_async_copy(m_ref.at[a : a + 19], M.at[a : a + 19], msem.at[a // 19])
        for a in (0, 19)
    ]
    for copy in loads:
        copy.start()
    lane = lanes_iota()

    def sweep(src, dst, row0, first):
        def body(x, _):
            for b in range(9):
                r = row0 + 8 * b
                new = sweep_block(x, r, src, dst, S, lane, True if first else None)
                for c in range(4):
                    dst[x, c, pl.ds(r, 8), :] = new[c]
            return 0

        return body

    loads[0].wait()
    lax.fori_loop(1, 18, sweep(M, A, 6, True), 0)
    loads[1].wait()
    lax.fori_loop(18, 37, sweep(M, A, 6, True), 0)
    lax.fori_loop(2, 36, sweep(A, B, 7, False), 0)

    def last(i, _):
        for b in range(8):
            r = 8 + 8 * b
            both = []
            for half in range(2):
                x = 3 + 2 * i + half
                new = sweep_block(x, r, B, None, S, lane)
                for c in range(4):
                    O[2 * i + half, c, pl.ds(r - 8, 8), :] = new[c]
                both.append([v * lax.rsqrt(v * v + 1.0) for v in new])
            for c in range(4):
                H[c, pl.ds(r - 8, 8), :] = both[0][c] + both[1][c]
        for yt in range(4):
            row = pl.multiple_of((i // 8) * 256 + yt * 64 + (i % 8) * 8, 8)
            for c in range(4):
                Q[pl.ds(row, 8), c * 128 : c * 128 + 128] = (
                    H[c, pl.ds(16 * yt, 8, stride=2), :] + H[c, pl.ds(16 * yt + 1, 8, stride=2), :]
                )
        for c in range(4):
            pltpu.make_async_copy(
                O.at[pl.ds(2 * i, 2), c],
                surf_ref.at[pl.ds(2 * i, 2), :, c * 128 : c * 128 + 128],
                osem.at[c],
            ).start()
        return 0

    lax.fori_loop(0, 16, last, 0)

    def iota(shape, dim):
        return lax.broadcasted_iota(jnp.int32, shape, dim)

    fine = iota((512, 128), 0) // 2
    col = iota((512, 128), 1)
    base = (col % 32) * 8 + (col // 32) * 2
    pools = [(fine == base + e).astype(f32) for e in range(2)]
    for b in range(8):
        block = Q[64 * b : 64 * b + 64, :]
        halves = [
            jnp.dot(block, pool, precision=HIGH, preferred_element_type=f32) for pool in pools
        ]
        turned = jnp.concatenate(halves, axis=0).T
        for h in range(4):
            C[32 * b : 32 * b + 32, 128 * h : 128 * h + 128] = turned[32 * h : 32 * h + 32, :]
    j = iota((512, 512), 1)
    order = (iota((512, 512), 0) == (j % 8) * 64 + j // 8).astype(f32)
    coarse = 0.5 - 0.0625 * jnp.dot(C[...], order, precision=HIGH, preferred_element_type=f32)
    tiles = route_ref.shape[1]
    route = route_ref[...]
    matches = (route == iota((nw, tiles), 0)).astype(f32)
    before = (iota((tiles, tiles), 0) < iota((tiles, tiles), 1)).astype(f32)
    earlier = jnp.dot(matches, before, precision=HIGH, preferred_element_type=f32)
    position = jnp.sum(earlier * matches, axis=0, keepdims=True).astype(jnp.int32)
    target = route * 24 + position
    matrix = (iota((nw * 24, tiles), 0) == target).astype(f32)
    packed = jnp.dot(matrix, coarse, precision=HIGH, preferred_element_type=f32)
    for d in range(nw):
        out_ref[d] = packed[24 * d : 24 * d + CAP, :]
    for c in range(4):
        pltpu.make_async_copy(O.at[:, c], surf_ref.at[:, :, c * 128 : c * 128 + 128], osem.at[c]).wait()


def sweeps(moved, route, nw):
    return pl.pallas_call(
        functools.partial(sweep_kernel, nw),
        out_shape=(
            jax.ShapeDtypeStruct((CX, CY, CZ), f32),
            jax.ShapeDtypeStruct((nw, CAP, 512), f32),
        ),
        in_specs=[pl.BlockSpec(memory_space=pl.ANY), pl.BlockSpec(memory_space=pltpu.VMEM)],
        out_specs=(pl.BlockSpec(memory_space=pl.ANY), pl.BlockSpec(memory_space=pltpu.VMEM)),
        scratch_shapes=[
            pltpu.VMEM(FIELD, f32),
            pltpu.VMEM(FIELD, f32),
            pltpu.VMEM(FIELD, f32),
            pltpu.VMEM(FIELD, f32),
            pltpu.VMEM((CX, 4, CY, 128), f32),
            pltpu.VMEM((4, CY, 128), f32),
            pltpu.VMEM((512, 512), f32),
            pltpu.VMEM((256, 512), f32),
            pltpu.SemaphoreType.DMA((2,)),
            pltpu.SemaphoreType.DMA((4,)),
        ],
        compiler_params=pltpu.CompilerParams(vmem_limit_bytes=60 << 20),
        name="sweeps",
    )(moved, route)


def exchange_kernel(nw, src, dst, own_sem, ssem, rsem):
    w = lax.axis_index("wide")
    own = pltpu.make_async_copy(src.at[w], dst.at[w], own_sem)
    own.start()
    barrier = pltpu.get_barrier_semaphore()

    def greet(i, _):
        pl.semaphore_signal(
            barrier,
            inc=1,
            device_id={"wide": lax.rem(w + i, nw)},
            device_id_type=pl.DeviceIdType.MESH,
        )
        return 0

    lax.fori_loop(1, nw, greet, 0)
    pl.semaphore_wait(barrier, nw - 1)

    def copy(i):
        to = lax.rem(w + i, nw)
        return pltpu.make_async_remote_copy(
            src_ref=src.at[to],
            dst_ref=dst.at[w],
            send_sem=ssem.at[i],
            recv_sem=rsem.at[i],
            device_id={"wide": to},
            device_id_type=pl.DeviceIdType.MESH,
        )

    def send(i, _):
        copy(i).start()
        return 0

    lax.fori_loop(1, nw, send, 0)

    def finish(i, _):
        copy(i).wait()
        return 0

    lax.fori_loop(1, nw, finish, 0)
    own.wait()


def exchange(outgoing, nw):
    return pl.pallas_call(
        functools.partial(exchange_kernel, nw),
        out_shape=jax.ShapeDtypeStruct(outgoing.shape, f32),
        in_specs=[pl.BlockSpec(memory_space=pl.ANY)],
        out_specs=pl.BlockSpec(memory_space=pl.ANY),
        scratch_shapes=[
            pltpu.SemaphoreType.DMA,
            pltpu.SemaphoreType.DMA((nw,)),
            pltpu.SemaphoreType.DMA((nw,)),
        ],
        compiler_params=pltpu.CompilerParams(collective_id=1, has_side_effects=True),
        name="exchange",
    )(outgoing)


def solution(mesh):
    nw, nn = mesh.shape["wide"], mesh.shape["narrow"]

    def on_device(level_set, velocity, box_owner):
        moved = advect(level_set, velocity, nw, nn)
        surface, outgoing = sweeps(moved, box_owner.reshape(1, -1), nw)
        slots = exchange(outgoing, nw)
        return surface, slots.reshape(1, 1, nw * CAP, 512)

    return jax.shard_map(
        on_device,
        mesh=mesh,
        in_specs=(
            P("wide", "narrow", None),
            P(None, "wide", "narrow", None),
            P("wide", "narrow", None, None),
        ),
        out_specs=(P("wide", "narrow", None), P("wide", "narrow", None, None)),
        check_vma=False,
    )
```

time: 265 us -> 108 us (0.41)
  other arithmetic: 123 us -> 0 us
  Pallas kernels: 0 us -> 103 us
  local copies, waits for them, and re-layouts: 77.9 us -> 4.62 us
  blocking collectives: 35.1 us -> 0 us
  starting transfers between devices: 14.3 us -> 0 us
  waiting for transfers between devices: 11.4 us -> 0 us
    pallas_call x0 -> x3, Pallas kernels: none -> 103 us  [the longest x1 44.4 us: advect(): pl.pallas_call(functools.partial(advect_kernel, nw, nn), out_shape=jax.Sh...]
    sub x7 -> x0, other arithmetic: 100 us -> none  [the longest x1 58.8 us: advect_from(): return field - change]
    all_to_all x1 -> x0, blocking collectives: 35.1 us -> none  [on_device(): lax.all_to_all(outgoing, 'wide', split_axis=0, concat_axis=0, tiled=True)]
    transpose x1 -> x0, local copies, waits for them, and re-layouts: 27.6 us -> none  [to_tiles(): return grouped.transpose(0, 2, 4, 1, 3, 5).reshape(-1, edge ** 3)]
    reshape x4 -> x1, local copies, waits for them, and re-layouts: 21.7 us -> 2.44 us  [on_device(): return (surface, slots.reshape(1, 1, nw * CAP, 512))]
    another operation x4 -> x0, local copies, waits for them, and re-layouts: 16.2 us -> none  [the longest x1 16 us: restrict(): tiles.reshape(leading + (half_edge, 2, half_edge, 2, half_edge, 2))]
    ppermute x8 -> x0, starting transfers between devices: 14.3 us -> none  [the longest x2 8.72 us: extended(): after = lax.ppermute(first, axis, down)]
    ppermute x8 -> x0, waiting for transfers between devices: 11.4 us -> none  [the longest x2 8.17 us: extended(): after = lax.ppermute(first, axis, down)]
  transfers between devices with their start and end apart: 8 -> 0, of which waited for: 4 -> 0; matrix products, arithmetic and copies ran while one was open for 9% -> 0% of each run, Pallas kernels for 0% -> 0%
where the time goes in v1:
time: 108 us
  Pallas kernels  103 us (95%)
  local copies, waits for them, and re-layouts  4.62 us (4%)
    pallas_call x1, Pallas kernels, advect(): pl.pallas_call(functools.partial(advect_kernel, nw, nn), out_shape=jax.Sh...  44.4 us
    pallas_call x1, Pallas kernels, exchange(): pl.pallas_call(functools.partial(exchange_kernel, nw), out_shape=jax.Shap...  31.6 us
    pallas_call x1, Pallas kernels, sweeps(): pl.pallas_call(functools.partial(sweep_kernel, nw), out_shape=(jax.ShapeD...  26.7 us
    reshape x1, local copies, waits for them, and re-layouts, on_device(): return (surface, slots.reshape(1, 1, nw * CAP, 512))  2.44 us
    unnamed x2, local copies, waits for them, and re-layouts  2.18 us

profile of v1, /device:TPU:1, one launch (start us, length us, event | category | flops | bytes accessed | tf_op | source)
XLA Modules:
  0.0 107.9 jit_solution(5625090446342111384)
XLA Ops:
  0.6 0.0 copy-start
  0.6 2.2 %copy-done = f32[32,64,512]{2,1,0:T(8,128)S(1)} copy-done((f32[32,64,512]{2,1,0:T(8,128)S(1)}, f32[32,64,512]{2,1,0:T(8,128)}, u32[]{:S(2)}) %copy-start) | copy-done | bytes 4194328
  2.8 44.4 %advect.1.m_ref = f32[38,4,80,128]{3,2,1,0:T(8,128)} custom-call(f32[32,64,512]{2,1,0:T(8,128)S(1)} %copy-done, bf16[3,32,64,512]{3,2,1,0:T(8,128)(2,1)} %v_ref.1), custom_call_target="tpu_custom_call" | custom-call | tf_op jit(solution)/shard_map/advect/pallas_call | solution.py:250
  47.2 26.7 %sweeps.1 = (f32[32,64,512]{2,1,0:T(8,128)}, f32[32,20,512]{2,1,0:T(8,128)}) custom-call(f32[38,4,80,128]{3,2,1,0:T(8,128)} %advect.1.m_ref, s32[1,256]{1,0:T(1,128)} %bitcast.1), custom_call_target="tpu_custom_call" | custom-call | tf_op jit(solution)/shard_map/sweeps/pallas_call | solution.py:398
  73.9 31.6 %exchange.1 = f32[32,20,512]{2,1,0:T(8,128)} custom-call(f32[32,20,512]{2,1,0:T(8,128)} %get-tuple-element.5.src), custom_call_target="tpu_custom_call" | custom-call | tf_op jit(solution)/shard_map/exchange/pallas_call | solution.py:467
  105.5 2.4 %reshape.11 = f32[1,1,640,512]{3,2,1,0:T(8,128)} reshape(f32[32,20,512]{2,1,0:T(8,128)} %exchange.1) | data formatting | bytes 2621440 | tf_op jit(solution)/shard_map/reshape | solution.py:489
Async XLA Ops:
  0.6 2.2 %copy-start = (f32[32,64,512]{2,1,0:T(8,128)S(1)}, f32[32,64,512]{2,1,0:T(8,128)}, u32[]{:S(2)}) copy-start(f32[32,64,512]{2,1,0:T(8,128)} %l_ref.1) | copy-start | bytes 12582916

commit v2 on v1

v2 whole, which is shorter than its diff:
```python
import functools

import jax
import jax.numpy as jnp
from jax import lax
from jax.experimental import pallas as pl
from jax.experimental.pallas import tpu as pltpu
from jax.sharding import PartitionSpec as P

f32 = jnp.float32
EPS = 0.75e-6
CX, CY, CZ = 32, 64, 512
CAP = 20
FIELD = (38, 4, 80, 128)


def lanes_iota():
    return lax.broadcasted_iota(jnp.int32, (8, 128), 1)


def lane_from(prev, cur, k, lane):
    return pltpu.roll(jnp.where(lane >= 128 - k, prev, cur), k, 1)


def lane_to(cur, nxt, k, lane):
    return pltpu.roll(jnp.where(lane < k, nxt, cur), 128 - k, 1)


def corr(E1, E2, E3, E4):
    E2s = 0.75 * E2
    E3s = 0.75 * E3
    t1 = E2 - E1
    S1 = t1 * t1 + (E2s * (t1 + E2) + EPS)
    t2 = E3 - E2
    S2 = t2 * t2 + (E2s * E3 + EPS)
    t3 = E3 - E4
    S3 = t3 * t3 + (E3s * (t3 + E3) + EPS)
    r1 = 1.0 / S1
    r2 = 1.0 / S2
    r3 = 1.0 / S3
    w1 = r1 * r1
    w2 = (6.0 * r2) * r2
    w3 = (3.0 * r3) * r3
    return (E2 + (E3 + E3)) - ((w1 + w1) * (t2 - t1) - w3 * (t2 + t3)) / (w1 + w2 + w3)


def upwind(u, dm, dp, qm2, qm1, q0, qp1, qp2):
    p = u > 0
    V3 = jnp.where(p, dm, dp)
    E1 = jnp.where(p, qm2, qp2)
    E2 = jnp.where(p, qm1, qp1)
    E4 = jnp.where(p, qp1, qm1)
    return u * V3 + (jnp.abs(u) * (1.0 / 6.0)) * corr(E1, E2, q0, E4)


def differences(fs):
    d = [fs[i + 1] - fs[i] for i in range(6)]
    q = [d[i + 1] - d[i] for i in range(5)]
    return (d[2], d[3], *q)


def advect_group(x, row, F, V, M):
    lane = lanes_iota()
    zero = jnp.zeros((8, 128), f32)
    for h in range(2):
        r = row + 8 * h + 8
        fc = [F[x + 3, c, pl.ds(r, 8), :] for c in range(4)]
        dm, dp, q = [], [], []
        for c in range(4):
            if c > 0:
                fm = lane_from(fc[c - 1], fc[c], 1, lane)
            else:
                fm = jnp.where(lane == 0, fc[0], pltpu.roll(fc[0], 1, 1))
            if c < 3:
                fp = lane_to(fc[c], fc[c + 1], 1, lane)
            else:
                fp = jnp.where(lane == 127, fc[3], pltpu.roll(fc[3], 127, 1))
            dm.append(fc[c] - fm)
            dp.append(fp - fc[c])
            q.append(dp[c] - dm[c])
        for c in range(4):
            u = V[:, x, pl.ds(row, 16), c * 128 : c * 128 + 128][:, 8 * h : 8 * h + 8].astype(f32)
            fx = [fc[c] if k == 3 else F[x + k, c, pl.ds(r, 8), :] for k in range(7)]
            acc = upwind(u[0], *differences(fx))
            fy = [fc[c] if k == 3 else F[x + 3, c, pl.ds(r + k - 3, 8), :] for k in range(7)]
            acc = acc + upwind(u[1], *differences(fy))
            qp = q[c - 1] if c > 0 else zero
            qn = q[c + 1] if c < 3 else zero
            acc = acc + upwind(
                u[2],
                dm[c],
                dp[c],
                lane_from(qp, q[c], 2, lane),
                lane_from(qp, q[c], 1, lane),
                q[c],
                lane_to(q[c], qn, 1, lane),
                lane_to(q[c], qn, 2, lane),
            )
            M[x + 3, c, pl.ds(r, 8), :] = fc[c] - acc


def pack_rows(field, buf):
    def body(k, _):
        for j in range(8):
            for c in range(4):
                for s, row in ((0, 8), (1, 69)):
                    buf[s, c, pl.ds(k * 24 + 3 * j, 3), :] = field[k * 8 + j + 3, c, row : row + 3, :]
        return 0

    lax.fori_loop(0, 4, body, 0)


def unpack_rows(field, buf):
    def body(k, _):
        for j in range(8):
            for c in range(4):
                for s, row in ((0, 5), (1, 72)):
                    field[k * 8 + j + 3, c, row : row + 3, :] = buf[s, c, pl.ds(k * 24 + 3 * j, 3), :]
        return 0

    lax.fori_loop(0, 4, body, 0)


def sweep_block(x, r, src, dst, S, lane, moved=None):
    fc = [src[x, c, pl.ds(r, 8), :] for c in range(4)]
    new = []
    for c in range(4):
        cur = fc[c]
        if moved is None:
            s = S[x, c, pl.ds(r, 8), :]
        else:
            s = (0.3 * cur) * lax.rsqrt(cur * cur + 1.0)
            S[x, c, pl.ds(r, 8), :] = s
        sg = jnp.where(s > 0, 1.0, -1.0)
        sc = sg * cur

        def term(lo, hi):
            e = sc - jnp.minimum(jnp.minimum(sg * lo, sg * hi), sc)
            return e * e

        G = term(src[x - 1, c, pl.ds(r, 8), :], src[x + 1, c, pl.ds(r, 8), :])
        G = G + term(src[x, c, pl.ds(r - 1, 8), :], src[x, c, pl.ds(r + 1, 8), :])
        if c > 0:
            lo = lane_from(fc[c - 1], cur, 1, lane)
        else:
            lo = jnp.where(lane == 0, cur, pltpu.roll(cur, 1, 1))
        if c < 3:
            hi = lane_to(cur, fc[c + 1], 1, lane)
        else:
            hi = jnp.where(lane == 127, cur, pltpu.roll(cur, 127, 1))
        G = G + term(lo, hi)
        root = G * lax.rsqrt(jnp.maximum(G, 1e-37))
        new.append(cur - s * (root - 1.0))
    return new


def iota(shape, dim):
    return lax.broadcasted_iota(jnp.int32, shape, dim)


def place_tiles(route_ref, X, nw):
    tiles = route_ref.shape[1]
    route = route_ref[...]
    matches = (route == iota((nw, tiles), 0)).astype(f32)
    before = (iota((tiles, tiles), 0) < iota((tiles, tiles), 1)).astype(f32)
    earlier = jnp.dot(
        matches.astype(jnp.bfloat16), before.astype(jnp.bfloat16), preferred_element_type=f32
    )
    position = jnp.sum(earlier * matches, axis=0, keepdims=True).astype(jnp.int32)
    target = route * 24 + position
    X[...] = (iota((nw * 24, tiles), 0) == target).astype(f32).astype(jnp.bfloat16)


def gather_tiles(Q, T, C):
    for c in range(4):
        T[c * 128 : c * 128 + 128, :] = Q[c].T
    lane = lanes_iota()
    for zv in range(4):
        part = [
            T[pl.ds(128 * zv + 2 * z, 8, stride=16), :] + T[pl.ds(128 * zv + 2 * z + 1, 8, stride=16), :]
            for z in range(8)
        ]
        for s in (1, 2, 4):
            bit = (lane & s) > 0
            for z in range(8):
                if z & s == 0:
                    a, b = part[z], part[z | s]
                    part[z] = jnp.where(bit, pltpu.roll(b, s, 1), a)
                    part[z | s] = jnp.where(bit, b, pltpu.roll(a, 128 - s, 1))
        for t in range(8):
            C[32 * t + 8 * zv : 32 * t + 8 * zv + 8, :] = 0.5 - 0.0625 * part[t]


def pack_tiles(X, C, G, nw):
    rest = C[...]
    packed = None
    for _ in range(3):
        term = rest.astype(jnp.bfloat16)
        rest = rest - term.astype(f32)
        product = jnp.dot(X[...], term, preferred_element_type=f32)
        packed = product if packed is None else packed + product
    for d in range(nw):
        G[d] = packed[24 * d : 24 * d + CAP, :]


def kernel(
    nw, nn, l_ref, v_ref, route_ref, surf_ref, out_ref,
    F, M, V, S, O, ys, yr, ys2, yr2, cr, H, Q, T, C, X, G,
    lsem, vsem, osem, own_sem, ssem, rsem, tsem, usem,
):
    w, n = lax.axis_index("wide"), lax.axis_index("narrow")
    left, right = lax.rem(w + nw - 1, nw), lax.rem(w + 1, nw)
    down, up = lax.rem(n + nn - 1, nn), lax.rem(n + 1, nn)
    lane = lanes_iota()

    loads = [
        pltpu.make_async_copy(
            l_ref.at[:, :, c * 128 : c * 128 + 128], F.at[3:35, c, 8:72, :], lsem.at[c]
        )
        for c in range(4)
    ]
    speeds = [
        pltpu.make_async_copy(v_ref.at[:, a:b], V.at[:, a:b], vsem.at[i])
        for i, (a, b) in enumerate(((3, 16), (0, 3), (16, 32)))
    ]
    for copy in loads + speeds:
        copy.start()

    barrier = pltpu.get_barrier_semaphore()

    def greet(a, b):
        pl.semaphore_signal(
            barrier, inc=1, device_id={"wide": a, "narrow": b}, device_id_type=pl.DeviceIdType.MESH
        )

    def greet_wide(i, _):
        greet(lax.rem(w + i, nw), n)
        return 0

    lax.fori_loop(1, nw, greet_wide, 0)
    for a in (left, w, right):
        for b in (down, up):
            greet(a, b)
    pl.semaphore_wait(barrier, nw - 1 + 6)

    def send(src, dst, k, a, b):
        return pltpu.make_async_remote_copy(
            src_ref=src,
            dst_ref=dst,
            send_sem=ssem.at[k],
            recv_sem=rsem.at[k],
            device_id={"wide": a, "narrow": b},
            device_id_type=pl.DeviceIdType.MESH,
        )

    def sides(field, sent, got, k):
        return (
            [
                send(field.at[3:6, :, 8:72, :], field.at[35:38, :, 8:72, :], k, left, n),
                send(field.at[32:35, :, 8:72, :], field.at[0:3, :, 8:72, :], k + 1, right, n),
            ],
            [
                send(sent.at[0], got.at[1], k + 2, w, down),
                send(sent.at[1], got.at[0], k + 3, w, up),
            ],
        )

    first_x, first_y = sides(F, ys, yr, 0)
    second_x, second_y = sides(M, ys2, yr2, 4)
    corners = [
        send(ys2.at[0, :, 0:16, :], cr.at[1, 1], 8, left, down),
        send(ys2.at[1, :, 0:16, :], cr.at[1, 0], 9, left, up),
        send(ys2.at[0, :, 80:96, :], cr.at[0, 1], 10, right, down),
        send(ys2.at[1, :, 80:96, :], cr.at[0, 0], 11, right, up),
    ]

    for copy in loads:
        copy.wait()
    for copy in first_x:
        copy.start()
    pack_rows(F, ys)
    for copy in first_y:
        copy.start()
    place_tiles(route_ref, X, nw)

    def inner(i, _):
        advect_group(3 + i // 2, pl.multiple_of(16 + 16 * (i % 2), 16), F, V, M)
        return 0

    def rims(i, _):
        advect_group(i // 2, pl.multiple_of(48 * (i % 2), 16), F, V, M)
        return 0

    def ends(i, _):
        k = i // 2
        advect_group(k + 26 * (k // 3), pl.multiple_of(16 + 16 * (i % 2), 16), F, V, M)
        return 0

    speeds[0].wait()
    lax.fori_loop(0, 26, inner, 0)
    speeds[1].wait()
    speeds[2].wait()
    for copy in first_x + first_y:
        copy.wait()
    unpack_rows(F, yr)
    lax.fori_loop(0, 64, rims, 0)
    pack_rows(M, ys2)
    for copy in second_y + corners:
        copy.start()
    lax.fori_loop(0, 12, ends, 0)
    for copy in second_x:
        copy.start()
    lax.fori_loop(26, 52, inner, 0)
    for copy in second_x + second_y + corners:
        copy.wait()
    unpack_rows(M, yr2)
    for xs in range(2):
        for ysd in range(2):
            for j in range(3):
                row = (5, 72)[ysd]
                at = (7, 0)[xs] + 3 * j
                for c in range(4):
                    M[35 * xs + j, c, row : row + 3, :] = cr[xs, ysd, c, at : at + 3, :]

    def sweep(src, dst, row0, first, count, planes):
        def body(i, _):
            x = planes(i)
            for b in range(9):
                r = row0 + 8 * b
                new = sweep_block(x, r, src, dst, S, lane, True if first else None)
                for c in range(4):
                    dst[x, c, pl.ds(r, 8), :] = new[c]
            return 0

        lax.fori_loop(0, count, body, 0)

    def two(start, count):
        return 2 * count, lambda i: start + lax.rem(i, count) + 16 * (i // count)

    def last_sweep(q):
        def body(i, _):
            tile, pair = i // 2, lax.rem(i, 2)
            x0 = 4 * q + 2 * pair + 16 * tile
            for b in range(8):
                both = []
                for half in range(2):
                    new = sweep_block(x0 + half + 3, 8 + 8 * b, M, None, S, lane)
                    for c in range(4):
                        O[x0 + half, c, 8 * b : 8 * b + 8, :] = new[c]
                    both.append([v * lax.rsqrt(v * v + 1.0) for v in new])
                for c in range(4):
                    H[c, 8 * b : 8 * b + 8, :] = both[0][c] + both[1][c]
            for yt in range(4):
                for c in range(4):
                    Q[c, pl.ds(pair * 64 + tile * 4 + yt, 8, stride=8), :] = (
                        H[c, pl.ds(16 * yt, 8, stride=2), :]
                        + H[c, pl.ds(16 * yt + 1, 8, stride=2), :]
                    )
            for c in range(4):
                pltpu.make_async_copy(
                    O.at[pl.ds(x0, 2), c],
                    surf_ref.at[pl.ds(x0, 2), :, c * 128 : c * 128 + 128],
                    osem.at[c],
                ).start()
            return 0

        lax.fori_loop(0, 4, body, 0)

    def tile_copy(q, i):
        to = lax.rem(w + i, nw)
        return pltpu.make_async_remote_copy(
            src_ref=G.at[q, to],
            dst_ref=out_ref.at[w, :, q * 128 : q * 128 + 128],
            send_sem=tsem.at[q, i],
            recv_sem=usem.at[q, i],
            device_id={"wide": to},
            device_id_type=pl.DeviceIdType.MESH,
        )

    own = []
    for q in range(4):
        if q == 0:
            sweep(M, F, 6, True, *two(1, 8))
            sweep(F, M, 7, False, *two(2, 6))
        elif q < 3:
            sweep(M, F, 6, True, *two(4 * q + 5, 4))
            sweep(F, M, 7, False, *two(4 * q + 4, 4))
        else:
            sweep(M, F, 6, True, 4, lambda i: i + 33)
            sweep(F, M, 7, False, 6, lambda i: i + 16 + 14 * ((i + 2) // 4))
        last_sweep(q)
        gather_tiles(Q, T, C)
        pack_tiles(X, C, G.at[q], nw)

        def start(i, _):
            tile_copy(q, i).start()
            return 0

        lax.fori_loop(1, nw, start, 0)
        own.append(
            pltpu.make_async_copy(
                G.at[q, w], out_ref.at[w, :, q * 128 : q * 128 + 128], own_sem.at[q]
            )
        )
        own[-1].start()

    for q in range(4):

        def finish(i, _):
            tile_copy(q, i).wait()
            return 0

        lax.fori_loop(1, nw, finish, 0)
        own[q].wait()
    for c in range(4):
        pltpu.make_async_copy(O.at[:, c], surf_ref.at[:, :, c * 128 : c * 128 + 128], osem.at[c]).wait()


def solution(mesh):
    nw, nn = mesh.shape["wide"], mesh.shape["narrow"]
    rows = pltpu.VMEM((2, 4, 96, 128), f32)
    dma = pltpu.SemaphoreType.DMA
    hbm = pl.BlockSpec(memory_space=pl.ANY)
    call = pl.pallas_call(
        functools.partial(kernel, nw, nn),
        out_shape=(
            jax.ShapeDtypeStruct((CX, CY, CZ), f32),
            jax.ShapeDtypeStruct((nw, CAP, 512), f32),
        ),
        in_specs=[hbm, hbm, pl.BlockSpec(memory_space=pltpu.VMEM)],
        out_specs=(hbm, hbm),
        scratch_shapes=[
            pltpu.VMEM(FIELD, f32),
            pltpu.VMEM(FIELD, f32),
            pltpu.VMEM((3, CX, CY, CZ), jnp.bfloat16),
            pltpu.VMEM(FIELD, f32),
            pltpu.VMEM((CX, 4, CY, 128), f32),
            rows,
            rows,
            rows,
            rows,
            pltpu.VMEM((2, 2, 4, 16, 128), f32),
            pltpu.VMEM((4, CY, 128), f32),
            pltpu.VMEM((4, 128, 128), f32),
            pltpu.VMEM((512, 128), f32),
            pltpu.VMEM((256, 128), f32),
            pltpu.VMEM((nw * 24, 256), jnp.bfloat16),
            pltpu.VMEM((4, nw, CAP, 128), f32),
            dma((4,)),
            dma((3,)),
            dma((4,)),
            dma((4,)),
            dma((12,)),
            dma((12,)),
            dma((4, nw)),
            dma((4, nw)),
        ],
        compiler_params=pltpu.CompilerParams(
            collective_id=0, has_side_effects=True, vmem_limit_bytes=60 << 20
        ),
        name="level_set_step",
    )

    def on_device(level_set, velocity, box_owner):
        surface, slots = call(level_set, velocity, box_owner.reshape(1, -1))
        return surface, slots.reshape(1, 1, nw * CAP, 512)

    return jax.shard_map(
        on_device,
        mesh=mesh,
        in_specs=(
            P("wide", "narrow", None),
            P(None, "wide", "narrow", None),
            P("wide", "narrow", None, None),
        ),
        out_specs=(P("wide", "narrow", None), P("wide", "narrow", None, None)),
        check_vma=False,
    )
```

time: 108 us -> 88 us (0.81)
  Pallas kernels: 103 us -> 79.8 us
  local copies, waits for them, and re-layouts: 4.62 us -> 7.35 us
    pallas_call x3 -> x1, Pallas kernels: 103 us -> 79.8 us  [on_device(): surface, slots = call(level_set, velocity, box_owner.reshape(1, -1))]
    unnamed x2 -> x1, local copies, waits for them, and re-layouts: 2.18 us -> 4.91 us
where the time goes in v2:
time: 88 us; the launch traced here: 87.8 us
  Pallas kernels  79.8 us (91%)
  local copies, waits for them, and re-layouts  7.35 us (8%)
    pallas_call x1, Pallas kernels, on_device(): surface, slots = call(level_set, velocity, box_owner.reshape(1, -1))  79.8 us
    unnamed x1, local copies, waits for them, and re-layouts  4.91 us
    reshape x1, local copies, waits for them, and re-layouts, on_device(): return (surface, slots.reshape(1, 1, nw * CAP, 512))  2.44 us

profile of v2, /device:TPU:1, one launch (start us, length us, event | category | flops | bytes accessed | tf_op | source)
XLA Modules:
  0.0 87.8 jit_solution(4569614682936029303)
XLA Ops:
  0.6 79.8 %level_set_step.1 = (f32[32,64,512]{2,1,0:T(8,128)}, f32[32,20,512]{2,1,0:T(8,128)}) custom-call(f32[32,64,512]{2,1,0:T(8,128)} %l_ref.1, bf16[3,32,64,512]{3,2,1,0:T(8,128)(2,1)} %v_ref.1, s32[1,256]{1,0:T(1,128)} %bitcast.1), custom_call_target="tpu_custom_call" | custom-call | tf_op jit(solution)/shard_map/level_set_step/pallas_call | solution.py:465
  80.5 2.4 %reshape.11 = f32[1,1,640,512]{3,2,1,0:T(8,128)} reshape(f32[32,20,512]{2,1,0:T(8,128)} %get-tuple-element.5) | data formatting | bytes 2621440 | tf_op jit(solution)/shard_map/reshape | solution.py:466
  82.9 4.9 %copy.6 = f32[32,64,512]{2,1,0:T(8,128)} copy(f32[32,64,512]{2,1,0:T(8,128)} %get-tuple-element.8) | data formatting | bytes 8388608

commit v3 on v2

--- a/solution.py
+++ b/solution.py
@@ -59,13 +59,10 @@
     return (d[2], d[3], *q)
 
 
-def advect_group(x, row, F, V, M):
+def third_differences(x, row, F, Z):
     lane = lanes_iota()
-    zero = jnp.zeros((8, 128), f32)
     for h in range(2):
-        r = row + 8 * h + 8
-        fc = [F[x + 3, c, pl.ds(r, 8), :] for c in range(4)]
-        dm, dp, q = [], [], []
+        fc = [F[x + 3, c, pl.ds(row + 8 * h + 8, 8), :] for c in range(4)]
         for c in range(4):
             if c > 0:
                 fm = lane_from(fc[c - 1], fc[c], 1, lane)
@@ -75,28 +72,48 @@
                 fp = lane_to(fc[c], fc[c + 1], 1, lane)
             else:
                 fp = jnp.where(lane == 127, fc[3], pltpu.roll(fc[3], 127, 1))
-            dm.append(fc[c] - fm)
-            dp.append(fp - fc[c])
-            q.append(dp[c] - dm[c])
+            dm = fc[c] - fm
+            Z[0, c, 8 * h : 8 * h + 8, :] = (fp - fc[c]) - dm
+            Z[1, c, 8 * h : 8 * h + 8, :] = dm
+
+
+def advect_group(x, row, F, V, M, Z):
+    lane = lanes_iota()
+    zero = jnp.zeros((8, 128), f32)
+    for h in range(2):
+        r = row + 8 * h + 8
+        q = [zero, *(Z[0, c, 8 * h : 8 * h + 8, :] for c in range(4)), zero]
         for c in range(4):
+            f = F[x + 3, c, pl.ds(r, 8), :]
             u = V[:, x, pl.ds(row, 16), c * 128 : c * 128 + 128][:, 8 * h : 8 * h + 8].astype(f32)
-            fx = [fc[c] if k == 3 else F[x + k, c, pl.ds(r, 8), :] for k in range(7)]
+            fx = [f if k == 3 else F[x + k, c, pl.ds(r, 8), :] for k in range(7)]
             acc = upwind(u[0], *differences(fx))
-            fy = [fc[c] if k == 3 else F[x + 3, c, pl.ds(r + k - 3, 8), :] for k in range(7)]
+            fy = [f if k == 3 else F[x + 3, c, pl.ds(r + k - 3, 8), :] for k in range(7)]
             acc = acc + upwind(u[1], *differences(fy))
-            qp = q[c - 1] if c > 0 else zero
-            qn = q[c + 1] if c < 3 else zero
+            dm = Z[1, c, 8 * h : 8 * h + 8, :]
+            qp, qc, qn = q[c : c + 3]
             acc = acc + upwind(
                 u[2],
-                dm[c],
-                dp[c],
-                lane_from(qp, q[c], 2, lane),
-                lane_from(qp, q[c], 1, lane),
-                q[c],
-                lane_to(q[c], qn, 1, lane),
-                lane_to(q[c], qn, 2, lane),
+                dm,
+                dm + qc,
+                lane_from(qp, qc, 2, lane),
+                lane_from(qp, qc, 1, lane),
+                qc,
+                lane_to(qc, qn, 1, lane),
+                lane_to(qc, qn, 2, lane),
             )
-            M[x + 3, c, pl.ds(r, 8), :] = fc[c] - acc
+            M[x + 3, c, pl.ds(r, 8), :] = f - acc
+
+
+def advect_groups(count, place, F, V, M, Z):
+    third_differences(*place(0), F, Z.at[0])
+
+    def body(i, _):
+        advect_group(*place(i), F, V, M, Z.at[lax.rem(i, 2)])
+        third_differences(*place(lax.rem(i + 1, count)), F, Z.at[lax.rem(i + 1, 2)])
+        return 0
+
+    lax.fori_loop(0, count, body, 0)
 
 
 def pack_rows(field, buf):
@@ -204,9 +221,9 @@
 
 
 def kernel(
-    nw, nn, l_ref, v_ref, route_ref, surf_ref, out_ref,
-    F, M, V, S, O, ys, yr, ys2, yr2, cr, H, Q, T, C, X, G,
-    lsem, vsem, osem, own_sem, ssem, rsem, tsem, usem,
+    nw, nn, l_ref, v_ref, route_ref, O, out_ref,
+    F, M, V, S, Z, ys, yr, ys2, yr2, cr, H, Q, T, C, X, G,
+    lsem, vsem, ssem, rsem, tsem, usem,
 ):
     w, n = lax.axis_index("wide"), lax.axis_index("narrow")
     left, right = lax.rem(w + nw - 1, nw), lax.rem(w + 1, nw)
@@ -282,35 +299,31 @@
     for copy in first_y:
         copy.start()
     place_tiles(route_ref, X, nw)
-
-    def inner(i, _):
-        advect_group(3 + i // 2, pl.multiple_of(16 + 16 * (i % 2), 16), F, V, M)
-        return 0
-
-    def rims(i, _):
-        advect_group(i // 2, pl.multiple_of(48 * (i % 2), 16), F, V, M)
-        return 0
-
-    def ends(i, _):
+    def inner(start):
+        return lambda i: (3 + (i + start) // 2, pl.multiple_of(16 + 16 * lax.rem(i + start, 2), 16))
+
+    def rims(i):
+        return i // 2, pl.multiple_of(48 * lax.rem(i, 2), 16)
+
+    def ends(i):
         k = i // 2
-        advect_group(k + 26 * (k // 3), pl.multiple_of(16 + 16 * (i % 2), 16), F, V, M)
-        return 0
+        return k + 26 * (k // 3), pl.multiple_of(16 + 16 * lax.rem(i, 2), 16)
 
     speeds[0].wait()
-    lax.fori_loop(0, 26, inner, 0)
+    advect_groups(26, inner(0), F, V, M, Z)
     speeds[1].wait()
     speeds[2].wait()
     for copy in first_x + first_y:
         copy.wait()
     unpack_rows(F, yr)
-    lax.fori_loop(0, 64, rims, 0)
+    advect_groups(64, rims, F, V, M, Z)
     pack_rows(M, ys2)
     for copy in second_y + corners:
         copy.start()
-    lax.fori_loop(0, 12, ends, 0)
+    advect_groups(12, ends, F, V, M, Z)
     for copy in second_x:
         copy.start()
-    lax.fori_loop(26, 52, inner, 0)
+    advect_groups(26, inner(26), F, V, M, Z)
     for copy in second_x + second_y + corners:
         copy.wait()
     unpack_rows(M, yr2)
@@ -356,28 +369,31 @@
                         H[c, pl.ds(16 * yt, 8, stride=2), :]
                         + H[c, pl.ds(16 * yt + 1, 8, stride=2), :]
                     )
-            for c in range(4):
-                pltpu.make_async_copy(
-                    O.at[pl.ds(x0, 2), c],
-                    surf_ref.at[pl.ds(x0, 2), :, c * 128 : c * 128 + 128],
-                    osem.at[c],
-                ).start()
             return 0
 
         lax.fori_loop(0, 4, body, 0)
 
-    def tile_copy(q, i):
-        to = lax.rem(w + i, nw)
+    steps = [
+        (dx, (r + i) % 4, r // 4)
+        for r in range(8)
+        for i, dx in enumerate((1, 3, 2, 0))
+        if (dx, (r + i) % 4, r // 4) != (0, 0, 0)
+    ]
+
+    def tile_copy(q, j):
+        dx, dz, dc = steps[j]
+        z, x, core = w // 8, lax.rem(w // 2, 4), lax.rem(w, 2)
+        to = lax.rem(z + dz, nw // 8) * 8 + lax.rem(x + dx, 4) * 2 + lax.rem(core + dc, 2)
         return pltpu.make_async_remote_copy(
             src_ref=G.at[q, to],
-            dst_ref=out_ref.at[w, :, q * 128 : q * 128 + 128],
-            send_sem=tsem.at[q, i],
-            recv_sem=usem.at[q, i],
+            dst_ref=out_ref.at[q, w],
+            send_sem=tsem.at[q, j],
+            recv_sem=usem.at[q, j],
             device_id={"wide": to},
             device_id_type=pl.DeviceIdType.MESH,
         )
 
-    own = []
+    copies = []
     for q in range(4):
         if q == 0:
             sweep(M, F, 6, True, *two(1, 8))
@@ -391,50 +407,54 @@
         last_sweep(q)
         gather_tiles(Q, T, C)
         pack_tiles(X, C, G.at[q], nw)
-
-        def start(i, _):
-            tile_copy(q, i).start()
-            return 0
-
-        lax.fori_loop(1, nw, start, 0)
-        own.append(
-            pltpu.make_async_copy(
-                G.at[q, w], out_ref.at[w, :, q * 128 : q * 128 + 128], own_sem.at[q]
-            )
+        here = [tile_copy(q, j) for j in range(nw - 1)]
+        out_ref[q, w] = G[q, w]
+        for copy in here:
+            copy.start()
+        copies += here
+
+    for copy in copies:
+        copy.wait()
+
+
+def finish_kernel(nw, field_ref, slots_ref, surf_ref, out_ref, W, osem, psem):
+    puts = [
+        pltpu.make_async_copy(field_ref.at[:, c], surf_ref.at[:, :, 128 * c : 128 * c + 128], osem.at[c])
+        for c in range(4)
+    ]
+    for copy in puts:
+        copy.start()
+    for q in range(4):
+        for d in range(nw):
+            W[q, CAP * d : CAP * d + CAP, :] = slots_ref[q, d]
+        puts.append(
+            pltpu.make_async_copy(W.at[q], out_ref.at[:, 128 * q : 128 * q + 128], psem.at[q])
         )
-        own[-1].start()
-
-    for q in range(4):
-
-        def finish(i, _):
-            tile_copy(q, i).wait()
-            return 0
-
-        lax.fori_loop(1, nw, finish, 0)
-        own[q].wait()
-    for c in range(4):
-        pltpu.make_async_copy(O.at[:, c], surf_ref.at[:, :, c * 128 : c * 128 + 128], osem.at[c]).wait()
+        puts[-1].start()
+    for copy in puts:
+        copy.wait()
 
 
 def solution(mesh):
     nw, nn = mesh.shape["wide"], mesh.shape["narrow"]
     rows = pltpu.VMEM((2, 4, 96, 128), f32)
     dma = pltpu.SemaphoreType.DMA
-    hbm = pl.BlockSpec(memory_space=pl.ANY)
+    hbm = pl.BlockSpec(memory_space=pltpu.HBM)
+    vmem = pl.BlockSpec(memory_space=pltpu.VMEM)
     call = pl.pallas_call(
         functools.partial(kernel, nw, nn),
         out_shape=(
-            jax.ShapeDtypeStruct((CX, CY, CZ), f32),
-            jax.ShapeDtypeStruct((nw, CAP, 512), f32),
+            pltpu.VMEM((CX, 4, CY, 128), f32),
+            pltpu.VMEM((4, nw, CAP, 128), f32),
         ),
-        in_specs=[hbm, hbm, pl.BlockSpec(memory_space=pltpu.VMEM)],
-        out_specs=(hbm, hbm),
+        in_specs=[hbm, hbm, vmem],
+        out_specs=(vmem, vmem),
         scratch_shapes=[
             pltpu.VMEM(FIELD, f32),
             pltpu.VMEM(FIELD, f32),
             pltpu.VMEM((3, CX, CY, CZ), jnp.bfloat16),
             pltpu.VMEM(FIELD, f32),
-            pltpu.VMEM((CX, 4, CY, 128), f32),
+            pltpu.VMEM((2, 2, 4, 16, 128), f32),
             rows,
             rows,
             rows,
@@ -448,21 +468,31 @@
             pltpu.VMEM((4, nw, CAP, 128), f32),
             dma((4,)),
             dma((3,)),
-            dma((4,)),
-            dma((4,)),
             dma((12,)),
             dma((12,)),
             dma((4, nw)),
             dma((4, nw)),
         ],
         compiler_params=pltpu.CompilerParams(
-            collective_id=0, has_side_effects=True, vmem_limit_bytes=60 << 20
+            collective_id=0, has_side_effects=True, vmem_limit_bytes=57 << 20
         ),
         name="level_set_step",
     )
+    finish = pl.pallas_call(
+        functools.partial(finish_kernel, nw),
+        out_shape=(
+            jax.ShapeDtypeStruct((CX, CY, CZ), f32),
+            jax.ShapeDtypeStruct((nw * CAP, 512), f32),
+        ),
+        in_specs=[vmem, vmem],
+        out_specs=(hbm, hbm),
+        scratch_shapes=[pltpu.VMEM((4, nw * CAP, 128), f32), dma((4,)), dma((4,))],
+        compiler_params=pltpu.CompilerParams(vmem_limit_bytes=16 << 20),
+        name="finish",
+    )
 
     def on_device(level_set, velocity, box_owner):
-        surface, slots = call(level_set, velocity, box_owner.reshape(1, -1))
+        surface, slots = finish(*call(level_set, velocity, box_owner.reshape(1, -1)))
         return surface, slots.reshape(1, 1, nw * CAP, 512)
 
     return jax.shard_map(

time: 88 us -> 77.5 us (0.88)
  local copies, waits for them, and re-layouts: 7.35 us -> 0 us
  Pallas kernels: 79.8 us -> 76.7 us
    unnamed x1 -> x0, local copies, waits for them, and re-layouts: 4.91 us -> none
    pallas_call x1 -> x2, Pallas kernels: 79.8 us -> 76.7 us  [the longest x1 74.3 us: on_device(): call(level_set, velocity, box_owner.reshape(1, -1))]
    reshape x1 -> x0, local copies, waits for them, and re-layouts: 2.44 us -> none  [on_device(): return (surface, slots.reshape(1, 1, nw * CAP, 512))]
where the time goes in v3:
time: 77.5 us; the launch traced here: 77.4 us
  Pallas kernels  76.7 us (99%)
    pallas_call x1, Pallas kernels, on_device(): call(level_set, velocity, box_owner.reshape(1, -1))  74.3 us
    pallas_call x1, Pallas kernels, on_device(): finish(*call(level_set, velocity, box_owner.reshape(1, -1)))  2.47 us

profile of v3, /device:TPU:1, one launch (start us, length us, event | category | flops | bytes accessed | tf_op | source)
XLA Modules:
  0.0 77.4 jit_solution(10380104044059817044)
XLA Ops:
  0.6 74.3 %level_set_step.1 = (f32[32,4,64,128]{3,2,1,0:T(8,128)S(1)}, f32[4,32,20,128]{3,2,1,0:T(8,128)S(1)}) custom-call(f32[32,64,512]{2,1,0:T(8,128)} %l_ref.1, bf16[3,32,64,512]{3,2,1,0:T(8,128)(2,1)} %v_ref.1, s32[1,256]{1,0:T(1,128)} %bitcast.2), custom_call_target="tpu_custom_call" | custom-call | tf_op jit(solution)/shard_map/level_set_step/pallas_call | solution.py:495
  74.9 2.5 %finish.1 = (f32[32,64,512]{2,1,0:T(8,128)}, f32[640,512]{1,0:T(8,128)}) custom-call(f32[32,4,64,128]{3,2,1,0:T(8,128)S(1)} %get-tuple-element.6.field_ref, f32[4,32,20,128]{3,2,1,0:T(8,128)S(1)} %get-tuple-element.7.slots_ref), custom_call_target="tpu_custom_call" | custom-call | tf_op jit(solution)/shard_map/finish/pallas_call | solution.py:495

commit v4 on v3

--- a/solution.py
+++ b/solution.py
@@ -59,7 +59,7 @@
     return (d[2], d[3], *q)
 
 
-def third_differences(x, row, F, Z):
+def third_differences(x, row, F, Z, Y):
     lane = lanes_iota()
     for h in range(2):
         fc = [F[x + 3, c, pl.ds(row + 8 * h + 8, 8), :] for c in range(4)]
@@ -75,9 +75,16 @@
             dm = fc[c] - fm
             Z[0, c, 8 * h : 8 * h + 8, :] = (fp - fc[c]) - dm
             Z[1, c, 8 * h : 8 * h + 8, :] = dm
-
-
-def advect_group(x, row, F, V, M, Z):
+    for c in range(4):
+        for b in range(3):
+            at = row + 6 + 8 * b
+            f = F[x + 3, c, pl.ds(at, 8), :]
+            Y[c, 8 * b : 8 * b + 8, :] = (F[x + 3, c, pl.ds(at + 1, 8), :] - f) - (
+                f - F[x + 3, c, pl.ds(at - 1, 8), :]
+            )
+
+
+def advect_group(x, row, F, V, M, Z, Y):
     lane = lanes_iota()
     zero = jnp.zeros((8, 128), f32)
     for h in range(2):
@@ -88,8 +95,12 @@
             u = V[:, x, pl.ds(row, 16), c * 128 : c * 128 + 128][:, 8 * h : 8 * h + 8].astype(f32)
             fx = [f if k == 3 else F[x + k, c, pl.ds(r, 8), :] for k in range(7)]
             acc = upwind(u[0], *differences(fx))
-            fy = [f if k == 3 else F[x + 3, c, pl.ds(r + k - 3, 8), :] for k in range(7)]
-            acc = acc + upwind(u[1], *differences(fy))
+            acc = acc + upwind(
+                u[1],
+                f - F[x + 3, c, pl.ds(r - 1, 8), :],
+                F[x + 3, c, pl.ds(r + 1, 8), :] - f,
+                *(Y[c, 8 * h + k : 8 * h + k + 8, :] for k in range(5)),
+            )
             dm = Z[1, c, 8 * h : 8 * h + 8, :]
             qp, qc, qn = q[c : c + 3]
             acc = acc + upwind(
@@ -105,12 +116,13 @@
             M[x + 3, c, pl.ds(r, 8), :] = f - acc
 
 
-def advect_groups(count, place, F, V, M, Z):
-    third_differences(*place(0), F, Z.at[0])
+def advect_groups(count, place, F, V, M, Z, Y):
+    third_differences(*place(0), F, Z.at[0], Y.at[0])
 
     def body(i, _):
-        advect_group(*place(i), F, V, M, Z.at[lax.rem(i, 2)])
-        third_differences(*place(lax.rem(i + 1, count)), F, Z.at[lax.rem(i + 1, 2)])
+        advect_group(*place(i), F, V, M, Z.at[lax.rem(i, 2)], Y.at[lax.rem(i, 2)])
+        nxt = lax.rem(i + 1, 2)
+        third_differences(*place(lax.rem(i + 1, count)), F, Z.at[nxt], Y.at[nxt])
         return 0
 
     lax.fori_loop(0, count, body, 0)
@@ -222,7 +234,7 @@
 
 def kernel(
     nw, nn, l_ref, v_ref, route_ref, O, out_ref,
-    F, M, V, S, Z, ys, yr, ys2, yr2, cr, H, Q, T, C, X, G,
+    F, M, V, S, Z, Y, ys, yr, ys2, yr2, cr, H, Q, T, C, X, G,
     lsem, vsem, ssem, rsem, tsem, usem,
 ):
     w, n = lax.axis_index("wide"), lax.axis_index("narrow")
@@ -310,20 +322,20 @@
         return k + 26 * (k // 3), pl.multiple_of(16 + 16 * lax.rem(i, 2), 16)
 
     speeds[0].wait()
-    advect_groups(26, inner(0), F, V, M, Z)
+    advect_groups(26, inner(0), F, V, M, Z, Y)
     speeds[1].wait()
     speeds[2].wait()
     for copy in first_x + first_y:
         copy.wait()
     unpack_rows(F, yr)
-    advect_groups(64, rims, F, V, M, Z)
+    advect_groups(64, rims, F, V, M, Z, Y)
     pack_rows(M, ys2)
     for copy in second_y + corners:
         copy.start()
-    advect_groups(12, ends, F, V, M, Z)
+    advect_groups(12, ends, F, V, M, Z, Y)
     for copy in second_x:
         copy.start()
-    advect_groups(26, inner(26), F, V, M, Z)
+    advect_groups(26, inner(26), F, V, M, Z, Y)
     for copy in second_x + second_y + corners:
         copy.wait()
     unpack_rows(M, yr2)
@@ -455,6 +467,7 @@
             pltpu.VMEM((3, CX, CY, CZ), jnp.bfloat16),
             pltpu.VMEM(FIELD, f32),
             pltpu.VMEM((2, 2, 4, 16, 128), f32),
+            pltpu.VMEM((2, 4, 24, 128), f32),
             rows,
             rows,
             rows,

time: 77.5 us -> 77.8 us (level)
  no operation moved by 1% of the time
where the time goes in v4:
time: 77.8 us; the launch traced here: 77.6 us
  Pallas kernels  77 us (99%)
    pallas_call x1, Pallas kernels, on_device(): call(level_set, velocity, box_owner.reshape(1, -1))  74.5 us
    pallas_call x1, Pallas kernels, on_device(): finish(*call(level_set, velocity, box_owner.reshape(1, -1)))  2.47 us

profile of v4, /device:TPU:1, one launch (start us, length us, event | category | flops | bytes accessed | tf_op | source)
XLA Modules:
  0.0 77.6 jit_solution(3247690868846170378)
XLA Ops:
  0.6 74.5 %level_set_step.1 = (f32[32,4,64,128]{3,2,1,0:T(8,128)S(1)}, f32[4,32,20,128]{3,2,1,0:T(8,128)S(1)}) custom-call(f32[32,64,512]{2,1,0:T(8,128)} %l_ref.1, bf16[3,32,64,512]{3,2,1,0:T(8,128)(2,1)} %v_ref.1, s32[1,256]{1,0:T(1,128)} %bitcast.2), custom_call_target="tpu_custom_call" | custom-call | tf_op jit(solution)/shard_map/level_set_step/pallas_call | solution.py:508
  75.2 2.5 %finish.1 = (f32[32,64,512]{2,1,0:T(8,128)}, f32[640,512]{1,0:T(8,128)}) custom-call(f32[32,4,64,128]{3,2,1,0:T(8,128)S(1)} %get-tuple-element.6.field_ref, f32[4,32,20,128]{3,2,1,0:T(8,128)S(1)} %get-tuple-element.7.slots_ref), custom_call_target="tpu_custom_call" | custom-call | tf_op jit(solution)/shard_map/finish/pallas_call | solution.py:508
